TPU v7x, 32 devices: a whole 2x2x4 slice. The times are simulated.
32 devices in a mesh: gx: 2 (over core), gy: 4 (over y, x), gz: 4 (over z).
Axes of the slice: x: 2, y: 2, z: 4, core: 2. Of those that a mesh axis runs over, the one named last changes fastest.
Arguments:
- block_values: bfloat16 [4, 64, 4, 6, 128, 128], P('gy', 'gx', 'gz'), as said below
- block_cols: int32 [4, 64, 4, 6], P('gy', 'gx', 'gz'), may hold values from 0 to 63, as said below
Outputs:
- purified: float32 [256, 32768], P(('gx', 'gy'), 'gz')
Inputs may be any that keep to these rules, and one draw needn't show every extreme that they name: block_cols[a, s, b, :] holds 6 distinct tile columns of panel b at which tile row a * 64 + s of P is nonzero; every tile column of a panel is listed by exactly 6 tile rows of each slab; the pattern is symmetric: tile (i, j) is listed exactly when tile (j, i) is. `block_values`: P is symmetric: the tile listed at (i, j) is the transpose of the tile listed at (j, i), and diagonal tiles are symmetric.
All inputs are finite; a program needn't handle non-finite values.
Results may differ from a plain program's by a relative error of at most 0.0033.
Values may be sent and summed in bfloat16 or wider, within the bound.
A program may use at most 128 MiB of HBM per device.

v0:
```python
import jax
import jax.numpy as jnp
from jax import lax
from jax.sharding import PartitionSpec as P

WIN = 1


def broadcast(value, axis, source):
    kept = jnp.where(lax.axis_index(axis) == source, value, 0).astype(value.dtype)
    return lax.psum(kept, axis)


def densify(left_tiles, left_columns, slab_tiles):
    onehot = (
        left_columns[:, :, None] == jnp.arange(slab_tiles, dtype=jnp.int32)[None, None, :]
    ).astype(jnp.bfloat16)
    densified = jnp.einsum("wkj,wkyx->wyjx", onehot, left_tiles, preferred_element_type=jnp.float32)
    tile_size = left_tiles.shape[2]
    return densified.astype(jnp.bfloat16).reshape(
        left_tiles.shape[0] * tile_size, slab_tiles, tile_size
    )


def product_one(left_panel, panel_tiles, panel_columns):
    summed = jnp.zeros(
        (left_panel.shape[0], panel_tiles.shape[0], panel_tiles.shape[2]), jnp.float32
    )
    for column_slot in range(panel_tiles.shape[1]):
        picked = jnp.take(left_panel, panel_columns[:, column_slot], axis=1)
        summed = summed + jnp.einsum(
            "rix,iyx->riy", picked, panel_tiles[:, column_slot], preferred_element_type=jnp.float32
        )
    return summed


def product_two(rounded, panel_tiles, panel_columns, panel_width):
    summed = jnp.zeros((rounded.shape[0], panel_width, panel_tiles.shape[3]), jnp.float32)
    for column_slot in range(panel_tiles.shape[1]):
        product = jnp.einsum(
            "rix,ixy->riy", rounded, panel_tiles[:, column_slot], preferred_element_type=jnp.float32
        )
        summed = summed.at[:, panel_columns[:, column_slot], :].add(product)
    return summed


def local(block_values, block_cols):
    tiles_here = block_values[0, :, 0]
    columns_here = block_cols[0, :, 0]
    tile_size = tiles_here.shape[2]
    slab_tiles = tiles_here.shape[0] * lax.axis_size("gx")
    left_tiles, left_columns = (
        broadcast(tiles_here[:WIN], "gy", 0),
        broadcast(columns_here[:WIN], "gy", 0),
    )
    left_panel = densify(left_tiles, left_columns, slab_tiles)
    height = left_panel.shape[0]
    on_diagonal = (lax.axis_index("gy") == lax.axis_index("gz")).astype(jnp.float32)
    panel_tiles, panel_columns = (
        lax.all_gather(tiles_here, "gx", axis=0, tiled=True),
        lax.all_gather(columns_here, "gx", axis=0, tiled=True),
    )
    partial_square = product_one(left_panel, panel_tiles, panel_columns)
    partial_square = partial_square.reshape(height, slab_tiles * tile_size)
    square = lax.psum(partial_square, "gz")
    square_low = square.astype(jnp.bfloat16).reshape(height, slab_tiles, tile_size)
    applied = product_two(square_low, panel_tiles, panel_columns, slab_tiles).reshape(
        lax.axis_size("gy") * (height // lax.axis_size("gy")), slab_tiles * tile_size
    )
    return lax.psum_scatter(
        3.0 * on_diagonal * square - 2.0 * applied, "gy", scatter_dimension=0, tiled=True
    )


def solution(mesh):
    in_specs = (P("gy", "gx", "gz", None, None, None), P("gy", "gx", "gz", None))
    out_specs = P(("gx", "gy"), "gz")
    return jax.shard_map(local, mesh=mesh, in_specs=in_specs, out_specs=out_specs, check_vma=False)
```

profile of v0, /device:TPU:0, one launch (start us, length us, event | category | flops | bytes accessed | tf_op | source)
XLA Modules:
  0.0 449.8 jit_solution(1277576746980991775)
XLA Ops:
  9.2 8.0 %copy.48 = bf16[1,32,1,6,128,128]{5,4,1,3,2,0:T(8,128)(2,1)} copy(bf16[1,32,1,6,128,128]{5,4,3,2,1,0:T(8,128)(2,1)} %param.4) | data formatting | bytes 12582912 | tf_op args[0]
  18.2 8.9 %psum.25 = s32[6]{0:T(128)S(1)} all-reduce(s32[6]{0:T(128)S(1)} %fusion.44), channel_id=1, replica_groups=mesh['gx'=2,'gy'=4,'gz'=4] {'gy'}, use_global_device_ids=true, to_apply=%region_1.2 | all-reduce | flops 6 | bytes 48 | tf_op jit(solution)/shard_map/psum | solution.py:11
  29.5 27.4 %all-reduce.3.cloned.1.call-done = bf16[6,128,128]{2,0,1:T(8,128)(2,1)} async-done(((bf16[6,128,128]{2,0,1:T(8,128)(2,1)}), bf16[6,128,128]{2,0,1:T(8,128)(2,1)}) %all-reduce.3.cloned.1.call-update) | async-done | bytes 196624 | tf_op jit(solution)/shard_map/psum | solution.py:11
  73.0 6.2 %fusion.1 = f32[64,128,128]{1,2,0:T(8,128)} fusion(bf16[64,128,128]{2,1,0:T(8,128)(2,1)} %gather_fusion.4, pred[64]{0:T(512)(128)(4,1)S(1)} %get-tuple-element.24, bf16[64,6,128,128]{3,2,0,1:T(8,128)(2,1)} %bitcast.77), kind=kOutput, calls=%fused_computation.21 | convolution fusion | flops 269484032 | bytes 8388672 | tf_op jit(solution)/shard_map/rix,iyx->riy/dot_general | solution.py:31
  79.1 6.0 %fusion.3 = f32[64,128,128]{1,2,0:T(8,128)} fusion(bf16[64,128,128]{2,1,0:T(8,128)(2,1)} %gather_fusion.3, pred[64]{0:T(512)(128)(4,1)S(1)} %get-tuple-element.25, bf16[64,6,128,128]{3,2,0,1:T(8,128)(2,1)} %bitcast.78), kind=kOutput, calls=%fused_computation.23 | convolution fusion | flops 269484032 | bytes 8388672 | tf_op jit(solution)/shard_map/rix,iyx->riy/dot_general | solution.py:31
  85.2 3.6 fusion.5
  88.8 3.6 fusion.7
  92.4 3.6 fusion.9
  96.0 10.1 %add_add_fusion = f32[64,128,128]{1,2,0:T(8,128)} fusion(f32[64,128,128]{1,2,0:T(8,128)} %fusion.1, f32[64,128,128]{1,2,0:T(8,128)} %fusion.3, f32[64,128,128]{1,2,0:T(8,128)} %fusion.5, f32[64,128,128]{1,2,0:T(8,128)} %fusion.9, f32[64,128,128]{1,2,0:T(8,128)} %fusion.7, bf16[64,128,128]{2,1,0:T(8,128)(2,1)S(1)} %copy-done.4, ...), kind=kOutput, calls=%fused_computation.13 | convolution fusion | flops 274726912 | bytes 29360640 | tf_op jit(solution)/shard_map/rix,iyx->riy/dot_general | solution.py:31
  106.4 154.9 %all-reduce.5.cloned.1.call-done = f32[128,8192]{0,1:T(8,128)} async-done(((f32[128,8192]{0,1:T(8,128)}), f32[128,8192]{0,1:T(8,128)}) %all-reduce.5.cloned.1.call-update) | async-done | bytes 4194320 | tf_op jit(solution)/shard_map/psum | solution.py:65
  263.8 4.5 %fusion.24 = f32[64,128,128]{2,1,0:T(8,128)} fusion(bf16[128,64,128]{0,2,1:T(8,128)(2,1)S(1)} %bitcast.71, bf16[64,6,128,128]{3,2,0,1:T(8,128)(2,1)} %bitcast.79), kind=kOutput, calls=%fused_computation.46 | convolution fusion | flops 268435456 | bytes 8388608 | tf_op jit(solution)/shard_map/rix,ixy->riy/dot_general | solution.py:40
  268.4 4.6 %fusion.23 = f32[64,128,128]{2,1,0:T(8,128)} fusion(bf16[128,64,128]{0,2,1:T(8,128)(2,1)S(1)} %bitcast.72, bf16[64,6,128,128]{3,2,0,1:T(8,128)(2,1)} %bitcast.80), kind=kOutput, calls=%fused_computation.45 | convolution fusion | flops 268435456 | bytes 8388608 | tf_op jit(solution)/shard_map/rix,ixy->riy/dot_general | solution.py:40
  275.8 2.8 fusion.26
  286.7 13.9 %scatter_fusion = f32[128,64,128]{2,0,1:T(8,128)} fusion(f32[128,64,128]{2,0,1:T(8,128)} %broadcast_in_dim.30, s32[64]{0:T(128)S(1)} %get-tuple-element.7, f32[64,128,128]{2,1,0:T(8,128)} %fusion.23), kind=kCustom, calls=%fused_computation.6 | custom fusion | flops 1048576 | bytes 12583168 | tf_op jit(solution)/shard_map/scatter-add | solution.py:43
  300.6 13.6 %scatter_fusion.1 = f32[128,64,128]{2,0,1:T(8,128)} fusion(f32[128,64,128]{2,0,1:T(8,128)} %scatter_fusion, s32[64]{0:T(128)S(1)} %get-tuple-element.8, f32[64,128,128]{2,1,0:T(8,128)} %fusion.24), kind=kCustom, calls=%fused_computation.7 | custom fusion | flops 1048576 | bytes 12583168 | tf_op jit(solution)/shard_map/scatter-add | solution.py:43
  314.2 13.6 %scatter_fusion.2 = f32[128,64,128]{2,0,1:T(8,128)} fusion(f32[128,64,128]{2,0,1:T(8,128)} %scatter_fusion.1, s32[64]{0:T(128)S(1)} %get-tuple-element.9, f32[64,128,128]{2,1,0:T(8,128)} %fusion.25), kind=kCustom, calls=%fused_computation.8 | custom fusion | flops 1048576 | bytes 12583168 | tf_op jit(solution)/shard_map/scatter-add | solution.py:43
  327.9 13.7 %scatter_fusion.3 = f32[128,64,128]{2,0,1:T(8,128)} fusion(f32[128,64,128]{2,0,1:T(8,128)} %scatter_fusion.2, s32[64]{0:T(128)S(1)} %get-tuple-element.10, f32[64,128,128]{2,1,0:T(8,128)} %fusion.26), kind=kCustom, calls=%fused_computation.9 | custom fusion | flops 1048576 | bytes 12583168 | tf_op jit(solution)/shard_map/scatter-add | solution.py:43
  341.6 13.7 %scatter_fusion.4 = f32[128,64,128]{2,0,1:T(8,128)} fusion(f32[128,64,128]{2,0,1:T(8,128)} %scatter_fusion.3, s32[64]{0:T(128)S(1)} %get-tuple-element.11, f32[64,128,128]{2,1,0:T(8,128)} %fusion.27), kind=kCustom, calls=%fused_computation.10 | custom fusion | flops 1048576 | bytes 12583168 | tf_op jit(solution)/shard_map/scatter-add | solution.py:43
  355.2 13.6 %scatter_fusion.5 = f32[128,64,128]{2,0,1:T(8,128)} fusion(f32[128,64,128]{2,0,1:T(8,128)} %scatter_fusion.4, s32[64]{0:T(128)S(1)} %get-tuple-element.6, f32[64,128,128]{2,1,0:T(8,128)} %fusion.28), kind=kCustom, calls=%fused_computation.11 | custom fusion | flops 1048576 | bytes 12583168 | tf_op jit(solution)/shard_map/scatter-add | solution.py:43
  368.9 4.7 %broadcast_multiply_fusion = f32[128,64,128]{2,0,1:T(8,128)} fusion(f32[128,64,128]{2,0,1:T(8,128)} %scatter_fusion.5), kind=kLoop, calls=%fused_computation.37 | loop fusion | flops 1048576 | bytes 8388608 | tf_op jit(solution)/shard_map/mul | solution.py:71
  373.6 5.6 %copy.60 = f32[128,64,128]{0,2,1:T(8,128)} copy(f32[128,64,128]{2,0,1:T(8,128)} %broadcast_multiply_fusion) | data formatting | bytes 8388608 | tf_op jit(solution)/shard_map/mul | solution.py:71
  379.2 5.8 %bitcast_subtract_fusion = f32[128,8192]{0,1:T(8,128)} fusion(f32[128,64,128]{0,2,1:T(8,128)} %copy.60, f32[128,8192]{0,1:T(8,128)} %all-reduce.5.cloned.1.call-done, f32[]{:T(128)S(6)} %mul_shard_map.3), kind=kLoop, calls=%fused_computation.12 | loop fusion | flops 2097152 | bytes 12582916 | tf_op jit(solution)/shard_map/sub | solution.py:71
  385.1 5.6 %copy.68 = f32[128,8192]{1,0:T(8,128)} copy(f32[128,8192]{0,1:T(8,128)} %bitcast_subtract_fusion) | data formatting | bytes 8388608
  390.7 51.9 %reduce-scatter.4.cloned.1.call-done = f32[32,8192]{1,0:T(8,128)} async-done(((f32[128,8192]{1,0:T(8,128)}), f32[32,8192]{1,0:T(8,128)}) %reduce-scatter.4.cloned.1.call-update) | async-done | bytes 1048592 | tf_op jit(solution)/shard_map/reduce_scatter | solution.py:70
  (60 shorter events, 34.9 us)
Async XLA Ops:
  7.4 49.5 %all-reduce.3.cloned.1.call-start = ((), (), s32[]{:S(2)}) async-start(), calls=%async_computation.1 | async-start | bytes 524288 | tf_op jit(solution)/shard_map/psum | solution.py:11
  9.2 63.8 %all-gather.4.cloned.1.call-start = ((), (), s32[]{:S(2)}) async-start(), calls=%async_computation.3 | async-start | bytes 18874368 | tf_op jit(solution)/shard_map/all_gather | solution.py:60
  17.3 0.7 copy-start.5
  17.3 244.0 %all-reduce.5.cloned.1.call-start = ((), (), s32[]{:S(2)}) async-start(), calls=%async_computation.2 | async-start | bytes 8388608 | tf_op jit(solution)/shard_map/psum | solution.py:65
  73.0 12.2 %copy-start = (bf16[1,64,1,6,128,128]{5,4,1,3,2,0:T(8,128)(2,1)S(1)}, bf16[1,64,1,6,128,128]{5,4,1,3,2,0:T(8,128)(2,1)}, u32[]{:S(2)}) copy-start(bf16[1,64,1,6,128,128]{5,4,1,3,2,0:T(8,128)(2,1)} %all-gather.4.cloned.1.call-done) | copy-start | bytes 37748740
  79.1 6.0 %copy-start.3 = (bf16[64,128,128]{2,1,0:T(8,128)(2,1)S(1)}, bf16[64,128,128]{2,1,0:T(8,128)(2,1)}, u32[]{:S(2)}) copy-start(bf16[64,128,128]{2,1,0:T(8,128)(2,1)} %gather_fusion.2) | copy-start | bytes 6291460
  85.2 3.6 copy-start.2
  88.8 3.6 copy-start.1
  92.4 3.6 copy-start.4
  106.1 336.5 %reduce-scatter.4.cloned.1.call-start = ((), (), s32[]{:S(2)}) async-start(), calls=%async_computation.4 | async-start | bytes 5242880 | tf_op jit(solution)/shard_map/reduce_scatter | solution.py:70
  261.3 11.7 %slice-start = ((s8[12582912]{0:T(1024)(128)(4,1)}), s8[4194304]{0:T(1024)(128)(4,1)S(1)}, s32[]{:S(2)}) async-start(s8[12582912]{0:T(1024)(128)(4,1)} %bitcast.85), calls=%async_computation.5 | async-start | bytes 8388608
  263.8 9.1 %slice-start.1 = ((s8[12582912]{0:T(1024)(128)(4,1)}), s8[4194304]{0:T(1024)(128)(4,1)S(1)}, s32[]{:S(2)}) async-start(s8[12582912]{0:T(1024)(128)(4,1)} %bitcast.85), calls=%async_computation.6 | async-start | bytes 8388608
  268.3 4.6 %slice-start.2 = ((s8[12582912]{0:T(1024)(128)(4,1)}), s8[4194304]{0:T(1024)(128)(4,1)S(1)}, s32[]{:S(2)}) async-start(s8[12582912]{0:T(1024)(128)(4,1)} %bitcast.85), calls=%async_computation.7 | async-start | bytes 8388608
Sparse Core Ops, SparseCore 0:
  11.1 45.7 all-reduce.2
  106.3 154.9 all-reduce.4
  390.8 51.7 reduce-scatter.3
Sparse Core Ops, SparseCore 1:
  17.4 27.3 all-gather.3
where the time goes:
time: 451 us; the launch traced here: 450 us
  waiting for transfers between devices  234 us (52%)
  other arithmetic  96.8 us (21%)
  matrix products  55.3 us (12%)
  local copies, waits for them, and re-layouts  37.7 us (8%)
  between operations  14.7 us (3%)
  blocking collectives  10.7 us (2%)
    psum x1, waiting for transfers between devices, local(): square = lax.psum(partial_square, 'gz')  155 us
    scatter-add x6, other arithmetic, product_two(): summed = summed.at[:, panel_columns[:, column_slot], :].add(product)  82.2 us
    reduce_scatter x1, waiting for transfers between devices, local(): lax.psum_scatter(3.0 * on_diagonal * square - 2.0 * applied, 'gy', scatte...  51.9 us
    dot_general x6, matrix products, product_one(): jnp.einsum('rix,iyx->riy', picked, panel_tiles[:, column_slot], preferred...  33.1 us
    psum x1, waiting for transfers between devices, broadcast(): return lax.psum(kept, axis)  27.4 us
    dot_general x6, matrix products, product_two(): jnp.einsum('rix,ixy->riy', rounded, panel_tiles[:, column_slot], preferre...  20.4 us
    unnamed x21, local copies, waits for them, and re-layouts  14.4 us
    gather x6, local copies, waits for them, and re-layouts, product_one(): picked = jnp.take(left_panel, panel_columns[:, column_slot], axis=1)  12.9 us
  transfers between devices with their start and end apart: 4, of which 3 were waited for; matrix products, arithmetic and copies ran while one was open for 6% of the time, Pallas kernels for 0%

commit v1 on v0

--- a/solution.py
+++ b/solution.py
@@ -8,7 +8,7 @@
 
 def broadcast(value, axis, source):
     kept = jnp.where(lax.axis_index(axis) == source, value, 0).astype(value.dtype)
-    return lax.psum(kept, axis)
+    return jnp.sum(lax.all_gather(kept, axis), axis=0)
 
 
 def densify(left_tiles, left_columns, slab_tiles):

time: 451 us -> 434 us (0.962)
  waiting for transfers between devices: 234 us -> 207 us
  blocking collectives: 10.7 us -> 23.5 us
    psum x1 -> x0, waiting for transfers between devices: 27.4 us -> none  [broadcast(): return lax.psum(kept, axis)]
    all_gather x0 -> x2, blocking collectives: none -> 21.5 us  [broadcast(): return jnp.sum(lax.all_gather(kept, axis), axis=0)]
    psum x1 -> x0, blocking collectives: 8.89 us -> none  [broadcast(): return lax.psum(kept, axis)]
    unnamed x21 -> x22, local copies, waits for them, and re-layouts: 14.4 us -> 14.5 us
  transfers between devices with their start and end apart: 4 -> 3, of which waited for: 3 -> 2; matrix products, arithmetic and copies ran while one was open for 6% -> 4% of each run, Pallas kernels for 0% -> 0%
where the time goes in v1:
time: 434 us; the launch traced here: 432 us
  waiting for transfers between devices  207 us (48%)
  other arithmetic  97 us (22%)
  matrix products  54.3 us (13%)
  local copies, waits for them, and re-layouts  36.8 us (8%)
  blocking collectives  23.5 us (5%)
  between operations  13.2 us (3%)
    psum x1, waiting for transfers between devices, local(): square = lax.psum(partial_square, 'gz')  155 us
    scatter-add x6, other arithmetic, product_two(): summed = summed.at[:, panel_columns[:, column_slot], :].add(product)  82.2 us
    reduce_scatter x1, waiting for transfers between devices, local(): lax.psum_scatter(3.0 * on_diagonal * square - 2.0 * applied, 'gy', scatte...  51.9 us
    dot_general x6, matrix products, product_one(): jnp.einsum('rix,iyx->riy', picked, panel_tiles[:, column_slot], preferred...  33.1 us
    all_gather x2, blocking collectives, broadcast(): return jnp.sum(lax.all_gather(kept, axis), axis=0)  21.5 us
    dot_general x6, matrix products, product_two(): jnp.einsum('rix,ixy->riy', rounded, panel_tiles[:, column_slot], preferre...  20.4 us
    unnamed x22, local copies, waits for them, and re-layouts  14.5 us
    gather x6, local copies, waits for them, and re-layouts, product_one(): picked = jnp.take(left_panel, panel_columns[:, column_slot], axis=1)  12.9 us
  transfers between devices with their start and end apart: 3, of which 2 were waited for; matrix products, arithmetic and copies ran while one was open for 4% of the time, Pallas kernels for 0%

profile of v1, /device:TPU:0, one launch (start us, length us, event | category | flops | bytes accessed | tf_op | source)
XLA Modules:
  0.0 432.4 jit_solution(15019416371879716149)
XLA Ops:
  6.5 8.0 %copy.48 = bf16[1,32,1,6,128,128]{5,4,1,3,2,0:T(8,128)(2,1)} copy(bf16[1,32,1,6,128,128]{5,4,3,2,1,0:T(8,128)(2,1)} %param.4) | data formatting | bytes 12582912 | tf_op args[0]
  15.4 9.4 %all-gather.1 = s32[4,1,1,6]{3,2,1,0:T(1,128)S(1)} all-gather(s32[1,1,1,6]{3,2,1,0:T(1,128)S(1)} %broadcast_select_fusion), channel_id=3, replica_groups=mesh['gx'=2,'gy'=4,'gz'=4] {'gy'}, dimensions={0}, use_global_device_ids=true | all-gather | bytes 120 | tf_op jit(solution)/shard_map/all_gather | solution.py:11
  25.9 12.1 %all-gather = bf16[4,1,1,6,128,128]{5,4,3,2,1,0:T(8,128)(2,1)S(1)} all-gather(bf16[1,1,1,6,128,128]{5,4,3,2,1,0:T(8,128)(2,1)S(1)} %slice_select_fusion), channel_id=2, replica_groups=mesh['gx'=2,'gy'=4,'gz'=4] {'gy'}, dimensions={0}, use_global_device_ids=true | all-gather | bytes 983040 | tf_op jit(solution)/shard_map/all_gather | solution.py:11
  55.8 6.2 %fusion.1 = f32[64,128,128]{1,2,0:T(8,128)} fusion(bf16[64,128,128]{2,1,0:T(8,128)(2,1)} %gather_fusion.4, pred[64]{0:T(512)(128)(4,1)S(1)} %get-tuple-element.25, bf16[64,6,128,128]{3,2,0,1:T(8,128)(2,1)} %bitcast.73), kind=kOutput, calls=%fused_computation.21 | convolution fusion | flops 269484032 | bytes 8388672 | tf_op jit(solution)/shard_map/rix,iyx->riy/dot_general | solution.py:31
  62.0 6.0 %fusion.3 = f32[64,128,128]{1,2,0:T(8,128)} fusion(bf16[64,128,128]{2,1,0:T(8,128)(2,1)} %gather_fusion.3, pred[64]{0:T(512)(128)(4,1)S(1)} %get-tuple-element.26, bf16[64,6,128,128]{3,2,0,1:T(8,128)(2,1)} %bitcast.74), kind=kOutput, calls=%fused_computation.23 | convolution fusion | flops 269484032 | bytes 8388672 | tf_op jit(solution)/shard_map/rix,iyx->riy/dot_general | solution.py:31
  68.0 3.6 fusion.5
  71.7 3.6 fusion.7
  75.3 3.6 fusion.9
  78.9 10.1 %add_add_fusion = f32[64,128,128]{1,2,0:T(8,128)} fusion(f32[64,128,128]{1,2,0:T(8,128)} %fusion.1, f32[64,128,128]{1,2,0:T(8,128)} %fusion.3, f32[64,128,128]{1,2,0:T(8,128)} %fusion.5, f32[64,128,128]{1,2,0:T(8,128)} %fusion.9, f32[64,128,128]{1,2,0:T(8,128)} %fusion.7, bf16[64,128,128]{2,1,0:T(8,128)(2,1)S(1)} %copy-done.4, ...), kind=kOutput, calls=%fused_computation.13 | convolution fusion | flops 274726912 | bytes 29360640 | tf_op jit(solution)/shard_map/rix,iyx->riy/dot_general | solution.py:31
  89.3 155.2 %all-reduce.2.cloned.1.call-done = f32[128,8192]{0,1:T(8,128)} async-done(((f32[128,8192]{0,1:T(8,128)}), f32[128,8192]{0,1:T(8,128)}) %all-reduce.2.cloned.1.call-update) | async-done | bytes 4194320 | tf_op jit(solution)/shard_map/psum | solution.py:65
  247.0 4.5 %fusion.24 = f32[64,128,128]{2,1,0:T(8,128)} fusion(bf16[128,64,128]{0,2,1:T(8,128)(2,1)S(1)} %bitcast.67, bf16[64,6,128,128]{3,2,0,1:T(8,128)(2,1)} %bitcast.75), kind=kOutput, calls=%fused_computation.46 | convolution fusion | flops 268435456 | bytes 8388608 | tf_op jit(solution)/shard_map/rix,ixy->riy/dot_general | solution.py:40
  251.5 4.6 %fusion.23 = f32[64,128,128]{2,1,0:T(8,128)} fusion(bf16[128,64,128]{0,2,1:T(8,128)(2,1)S(1)} %bitcast.68, bf16[64,6,128,128]{3,2,0,1:T(8,128)(2,1)} %bitcast.76), kind=kOutput, calls=%fused_computation.45 | convolution fusion | flops 268435456 | bytes 8388608 | tf_op jit(solution)/shard_map/rix,ixy->riy/dot_general | solution.py:40
  259.0 2.8 fusion.26
  269.9 14.0 %scatter_fusion = f32[128,64,128]{2,0,1:T(8,128)} fusion(f32[128,64,128]{2,0,1:T(8,128)} %broadcast_in_dim.30, s32[64]{0:T(128)S(1)} %get-tuple-element.7, f32[64,128,128]{2,1,0:T(8,128)} %fusion.23), kind=kCustom, calls=%fused_computation.6 | custom fusion | flops 1048576 | bytes 12583168 | tf_op jit(solution)/shard_map/scatter-add | solution.py:43
  283.8 13.6 %scatter_fusion.1 = f32[128,64,128]{2,0,1:T(8,128)} fusion(f32[128,64,128]{2,0,1:T(8,128)} %scatter_fusion, s32[64]{0:T(128)S(1)} %get-tuple-element.8, f32[64,128,128]{2,1,0:T(8,128)} %fusion.24), kind=kCustom, calls=%fused_computation.7 | custom fusion | flops 1048576 | bytes 12583168 | tf_op jit(solution)/shard_map/scatter-add | solution.py:43
  297.5 13.6 %scatter_fusion.2 = f32[128,64,128]{2,0,1:T(8,128)} fusion(f32[128,64,128]{2,0,1:T(8,128)} %scatter_fusion.1, s32[64]{0:T(128)S(1)} %get-tuple-element.9, f32[64,128,128]{2,1,0:T(8,128)} %fusion.25), kind=kCustom, calls=%fused_computation.8 | custom fusion | flops 1048576 | bytes 12583168 | tf_op jit(solution)/shard_map/scatter-add | solution.py:43
  311.1 13.7 %scatter_fusion.3 = f32[128,64,128]{2,0,1:T(8,128)} fusion(f32[128,64,128]{2,0,1:T(8,128)} %scatter_fusion.2, s32[64]{0:T(128)S(1)} %get-tuple-element.10, f32[64,128,128]{2,1,0:T(8,128)} %fusion.26), kind=kCustom, calls=%fused_computation.9 | custom fusion | flops 1048576 | bytes 12583168 | tf_op jit(solution)/shard_map/scatter-add | solution.py:43
  324.8 13.7 %scatter_fusion.4 = f32[128,64,128]{2,0,1:T(8,128)} fusion(f32[128,64,128]{2,0,1:T(8,128)} %scatter_fusion.3, s32[64]{0:T(128)S(1)} %get-tuple-element.11, f32[64,128,128]{2,1,0:T(8,128)} %fusion.27), kind=kCustom, calls=%fused_computation.10 | custom fusion | flops 1048576 | bytes 12583168 | tf_op jit(solution)/shard_map/scatter-add | solution.py:43
  338.4 13.6 %scatter_fusion.5 = f32[128,64,128]{2,0,1:T(8,128)} fusion(f32[128,64,128]{2,0,1:T(8,128)} %scatter_fusion.4, s32[64]{0:T(128)S(1)} %get-tuple-element.6, f32[64,128,128]{2,1,0:T(8,128)} %fusion.28), kind=kCustom, calls=%fused_computation.11 | custom fusion | flops 1048576 | bytes 12583168 | tf_op jit(solution)/shard_map/scatter-add | solution.py:43
  352.1 4.7 %broadcast_multiply_fusion = f32[128,64,128]{2,0,1:T(8,128)} fusion(f32[128,64,128]{2,0,1:T(8,128)} %scatter_fusion.5), kind=kLoop, calls=%fused_computation.37 | loop fusion | flops 1048576 | bytes 8388608 | tf_op jit(solution)/shard_map/mul | solution.py:71
  356.8 5.6 %copy.60 = f32[128,64,128]{0,2,1:T(8,128)} copy(f32[128,64,128]{2,0,1:T(8,128)} %broadcast_multiply_fusion) | data formatting | bytes 8388608 | tf_op jit(solution)/shard_map/mul | solution.py:71
  362.4 5.8 %bitcast_subtract_fusion = f32[128,8192]{0,1:T(8,128)} fusion(f32[128,64,128]{0,2,1:T(8,128)} %copy.60, f32[128,8192]{0,1:T(8,128)} %all-reduce.2.cloned.1.call-done, f32[]{:T(128)S(6)} %mul_shard_map.3), kind=kLoop, calls=%fused_computation.12 | loop fusion | flops 2097152 | bytes 12582916 | tf_op jit(solution)/shard_map/sub | solution.py:71
  368.3 5.6 %copy.68 = f32[128,8192]{1,0:T(8,128)} copy(f32[128,8192]{0,1:T(8,128)} %bitcast_subtract_fusion) | data formatting | bytes 8388608
  373.9 51.9 %reduce-scatter.4.cloned.1.call-done = f32[32,8192]{1,0:T(8,128)} async-done(((f32[128,8192]{1,0:T(8,128)}), f32[32,8192]{1,0:T(8,128)}) %reduce-scatter.4.cloned.1.call-update) | async-done | bytes 1048592 | tf_op jit(solution)/shard_map/reduce_scatter | solution.py:70
  (59 shorter events, 33.4 us)
Async XLA Ops:
  6.5 49.3 %all-gather.6.cloned.1.call-start = ((), (), s32[]{:S(2)}) async-start(), calls=%async_computation.2 | async-start | bytes 18874368 | tf_op jit(solution)/shard_map/all_gather | solution.py:60
  14.6 0.7 copy-start.5
  14.6 229.8 %all-reduce.2.cloned.1.call-start = ((), (), s32[]{:S(2)}) async-start(), calls=%async_computation.1 | async-start | bytes 8388608 | tf_op jit(solution)/shard_map/psum | solution.py:65
  55.8 12.2 %copy-start = (bf16[1,64,1,6,128,128]{5,4,1,3,2,0:T(8,128)(2,1)S(1)}, bf16[1,64,1,6,128,128]{5,4,1,3,2,0:T(8,128)(2,1)}, u32[]{:S(2)}) copy-start(bf16[1,64,1,6,128,128]{5,4,1,3,2,0:T(8,128)(2,1)} %all-gather.6.cloned.1.call-done) | copy-start | bytes 37748740
  62.0 6.0 %copy-start.1 = (bf16[64,128,128]{2,1,0:T(8,128)(2,1)S(1)}, bf16[64,128,128]{2,1,0:T(8,128)(2,1)}, u32[]{:S(2)}) copy-start(bf16[64,128,128]{2,1,0:T(8,128)(2,1)} %gather_fusion.2) | copy-start | bytes 6291460
  68.0 3.6 copy-start.2
  71.6 3.6 copy-start.3
  75.3 3.6 copy-start.4
  89.0 336.9 %reduce-scatter.4.cloned.1.call-start = ((), (), s32[]{:S(2)}) async-start(), calls=%async_computation.3 | async-start | bytes 5242880 | tf_op jit(solution)/shard_map/reduce_scatter | solution.py:70
  244.4 11.7 %slice-start = ((s8[12582912]{0:T(1024)(128)(4,1)}), s8[4194304]{0:T(1024)(128)(4,1)S(1)}, s32[]{:S(2)}) async-start(s8[12582912]{0:T(1024)(128)(4,1)} %bitcast.81), calls=%async_computation.4 | async-start | bytes 8388608
  247.0 9.1 %slice-start.1 = ((s8[12582912]{0:T(1024)(128)(4,1)}), s8[4194304]{0:T(1024)(128)(4,1)S(1)}, s32[]{:S(2)}) async-start(s8[12582912]{0:T(1024)(128)(4,1)} %bitcast.81), calls=%async_computation.5 | async-start | bytes 8388608
  251.5 4.6 %slice-start.2 = ((s8[12582912]{0:T(1024)(128)(4,1)}), s8[4194304]{0:T(1024)(128)(4,1)S(1)}, s32[]{:S(2)}) async-start(s8[12582912]{0:T(1024)(128)(4,1)} %bitcast.81), calls=%async_computation.6 | async-start | bytes 8388608
Sparse Core Ops, SparseCore 0:
  14.7 27.4 all-gather.5
  89.1 155.2 all-reduce.1
  374.1 51.7 reduce-scatter.3
